TPU v7x, 32 devices: a whole 2x2x4 slice. The times are simulated.
32 devices in a mesh: panels: 32 (over z, y, x, core).
Axes of the slice: x: 2, y: 2, z: 4, core: 2. Of those that a mesh axis runs over, the one named last changes fastest.
Arguments:
- excitation: bfloat16 [64, 131072], P(None, 'panels'), may hold values from -6 to 6
- near_tiles: bfloat16 [512, 5, 256, 256], P('panels'), may hold values from -0.15625 to 0.15625
- near_offset: int32 [512, 5], P('panels'), may hold values from -16 to 16, as said below
- near_count: int32 [512], P('panels'), may hold values from 1 to 5, as said below
- far_src: int32 [32, 16], replicated, may hold values from 0 to 31, as said below
- far_count: int32 [32], replicated, may hold values from 1 to 16
- source_factor: bfloat16 [16, 32, 131072], P(None, None, 'panels'), may hold values from -0.09375 to 0.09375
- target_factor: bfloat16 [16, 32, 131072], P(None, None, 'panels'), may hold values from -0.25 to 0.25
Outputs:
- krylov: float32 [5, 64, 131072], P(None, None, 'panels')
Inputs may be any that keep to these rules, and one draw needn't show every extreme that they name: `near_offset`: offsets within one leaf are distinct. `near_count`: some leaf has 5 live slots. `far_src`: within a row the entries are distinct and never the row itself. Counting live slots only, every block row is the source of at most 16 far blocks, and some block row of exactly 16.
All inputs are finite; a program needn't handle non-finite values.
Results may differ from a plain program's by a relative error of at most 0.0095.
Values may be sent and summed in bfloat16 or wider, within the bound.
A program may use at most 128 MiB of HBM per device.

v0:
```python
import functools

import jax
import jax.numpy as jnp
from jax import lax
from jax.experimental import pallas as pl
from jax.experimental.pallas import tpu as pltpu
from jax.sharding import PartitionSpec as P

ITERS = 5
MESH = pl.DeviceIdType.MESH
NT = (((1,), (1,)), ((), ()))


def kernel(
    n,
    idx_ref,
    field_hbm,
    leaves_hbm,
    near_hbm,
    src_hbm,
    tgt_hbm,
    out_hbm,
    near,
    src,
    tgt,
    field,
    ext_a,
    ext_b,
    recv_a,
    recv_b,
    outg_a,
    outg_b,
    cbuf,
    gin,
    stage_a,
    stage_b,
    load_sem,
    out_sem,
    halo_send,
    halo_recv,
    far_send,
    far_recv,
):
    me = lax.axis_index("panels")
    right, left = lax.rem(me + 1, n), lax.rem(me + n - 1, n)
    leaves, excite, leaf = leaves_hbm.shape
    slots = near_hbm.shape[0] // leaves
    far_slots, pack, _ = cbuf.shape
    far_slots -= 1
    rank = src.shape[0] // far_slots
    panels = leaves * leaf
    groups = 4 if leaves % 4 == 0 else 1
    size = leaves // groups
    exts, recvs, outgs, stages = (ext_a, ext_b), (recv_a, recv_b), (outg_a, outg_b), (stage_a, stage_b)

    loads = [
        pltpu.make_async_copy(field_hbm, field, load_sem.at[0]),
        pltpu.make_async_copy(leaves_hbm, ext_a.at[pl.ds(leaves, leaves)], load_sem.at[1]),
        pltpu.make_async_copy(src_hbm, src, load_sem.at[2]),
        pltpu.make_async_copy(tgt_hbm, tgt, load_sem.at[3]),
        pltpu.make_async_copy(near_hbm, near, load_sem.at[4]),
    ]
    for load in loads:
        load.start()

    for ext in exts:
        ext[3 * leaves] = jnp.zeros((excite, leaf), jnp.bfloat16)
    for recv in recvs:
        recv[n] = jnp.zeros((pack, 2 * excite), jnp.bfloat16)
        recv[me] = jnp.zeros((pack, 2 * excite), jnp.bfloat16)
    cbuf[far_slots] = jnp.zeros((pack, 2 * excite), jnp.bfloat16)

    barrier = pltpu.get_barrier_semaphore()

    @pl.loop(1, n)
    def _(d):
        pl.semaphore_signal(barrier, inc=1, device_id=(lax.rem(me + d, n),), device_id_type=MESH)

    pl.semaphore_wait(barrier, n - 1)

    def halo(k, g, side):
        ext = exts[k % 2]
        base = 0 if side == 0 else 2 * leaves
        return pltpu.make_async_remote_copy(
            src_ref=ext.at[pl.ds(leaves + g * size, size)],
            dst_ref=ext.at[pl.ds(base + g * size, size)],
            send_sem=halo_send.at[k % 2, side, g],
            recv_sem=halo_recv.at[k % 2, side, g],
            device_id=(right if side == 0 else left,),
            device_id_type=MESH,
        )

    def block(k, d):
        peer = lax.rem(me + d, n)
        return pltpu.make_async_remote_copy(
            src_ref=outgs[k % 2].at[peer],
            dst_ref=recvs[k % 2].at[me],
            send_sem=far_send.at[k % 2, d],
            recv_sem=far_recv.at[k % 2, d],
            device_id=(peer,),
            device_id_type=MESH,
        )

    loads[1].wait()
    for g in range(groups):
        halo(0, g, 0).start()
        halo(0, g, 1).start()
    loads[0].wait()
    loads[2].wait()

    half = src.shape[0] // 2
    rows_half = half // rank
    for k in range(ITERS):
        ext, recv, outg, stage = exts[k % 2], recvs[k % 2], outgs[k % 2], stages[k % 2]

        @pl.loop(0, 2)
        def _(h):
            part = lax.dot_general(
                src[pl.ds(pl.multiple_of(h * half, half), half), :],
                field[...],
                NT,
                preferred_element_type=jnp.float32,
            )
            part = part.reshape(rows_half, 2, pack, excite)
            part = jnp.concatenate([part[:, 0], part[:, 1]], axis=2)
            cbuf[pl.ds(h * rows_half, rows_half)] = part.astype(jnp.bfloat16)

        @pl.loop(0, n)
        def _(t):
            outg[t] = cbuf[idx_ref[leaves * slots + t]]

        @pl.loop(1, n)
        def _(d):
            block(k, d).start()

        if k >= 2:
            pltpu.make_async_copy(stage, out_hbm.at[k - 2], out_sem.at[k % 2]).wait()

        @pl.loop(1, n)
        def _(d):
            block(k, d).wait()

        for j in range(far_slots):
            got = recv[idx_ref[leaves * slots + n + j]].astype(jnp.float32)
            gin[pl.ds(j * rank, pack), :] = got[:, :excite]
            gin[pl.ds(j * rank + pack, pack), :] = got[:, excite:]
        coef = gin[...].T.astype(jnp.bfloat16)
        if k == 0:
            loads[3].wait()

        @pl.loop(0, groups)
        def _(g):
            cols = pl.ds(pl.multiple_of(g * size * leaf, size * leaf), size * leaf)
            stage[:, cols] = jnp.dot(coef, tgt[:, cols], preferred_element_type=jnp.float32)

        if k == 0:
            loads[4].wait()
        for g in range(groups):
            halo(k, g, 0).wait()
            halo(k, g, 1).wait()

        @pl.loop(0, groups)
        def _(g):
            for u in range(size):
                i = g * size + u
                cols = pl.ds(pl.multiple_of(i * leaf, leaf), leaf)
                total = stage[:, cols]
                for j in range(slots):
                    total += lax.dot_general(
                        ext[idx_ref[i * slots + j]],
                        near[i * slots + j],
                        NT,
                        preferred_element_type=jnp.float32,
                    )
                stage[:, cols] = total
                if k < ITERS - 1:
                    rounded = total.astype(jnp.bfloat16)
                    field[:, cols] = rounded
                    exts[(k + 1) % 2][leaves + i] = rounded
            if k < ITERS - 1:

                @pl.when(g > 0)
                def _():
                    halo(k + 1, g - 1, 0).start()
                    halo(k + 1, g - 1, 1).start()

        if k < ITERS - 1:
            halo(k + 1, groups - 1, 0).start()
            halo(k + 1, groups - 1, 1).start()
        pltpu.make_async_copy(stage, out_hbm.at[k], out_sem.at[k % 2]).start()
    for k in range(max(ITERS - 2, 0), ITERS):
        pltpu.make_async_copy(stages[k % 2], out_hbm.at[k], out_sem.at[k % 2]).wait()


def shards(n, excitation, near_tiles, near_offset, near_count, far_src, far_count, source_factor, target_factor):
    excite, panels = excitation.shape
    leaves, slots, leaf, _ = near_tiles.shape
    far_slots, rank, _ = source_factor.shape
    me = lax.axis_index("panels")
    ints = jnp.int32

    own = jnp.arange(leaves, dtype=ints)[:, None] + leaves + near_offset
    near_idx = jnp.where(jnp.arange(slots, dtype=ints)[None, :] < near_count[:, None], own, 3 * leaves)
    live = jnp.arange(far_slots, dtype=ints)[None, :] < far_count[:, None]
    has = jnp.sum(((far_src == me) & live).astype(ints), axis=1)
    rows = jnp.arange(n, dtype=ints)
    before = jnp.sum(jnp.where(rows[None, :] < rows[:, None], has[None, :], 0), axis=1)
    send_idx = jnp.where(has > 0, before, far_slots)
    my_src = lax.dynamic_index_in_dim(far_src, me, 0, keepdims=False)
    my_live = lax.dynamic_index_in_dim(live, me, 0, keepdims=False)
    recv_idx = jnp.where(my_live, my_src, n)
    idx = jnp.concatenate([near_idx.reshape(-1), send_idx, recv_idx]).astype(ints)
    leaf_field = excitation.reshape(excite, leaves, leaf).transpose(1, 0, 2)

    bf, f32 = jnp.bfloat16, jnp.float32
    groups = 4 if leaves % 4 == 0 else 1
    hbm = pl.BlockSpec(memory_space=pl.ANY)
    return pl.pallas_call(
        functools.partial(kernel, n),
        out_shape=jax.ShapeDtypeStruct((ITERS, excite, panels), f32),
        in_specs=[pl.BlockSpec(memory_space=pltpu.SMEM)] + [hbm] * 5,
        out_specs=hbm,
        scratch_shapes=[
            pltpu.VMEM((leaves * slots, leaf, leaf), bf),
            pltpu.VMEM((far_slots * rank, panels), bf),
            pltpu.VMEM((far_slots * rank, panels), bf),
            pltpu.VMEM((excite, panels), bf),
            pltpu.VMEM((3 * leaves + 1, excite, leaf), bf),
            pltpu.VMEM((3 * leaves + 1, excite, leaf), bf),
            pltpu.VMEM((n + 1, rank // 2, 2 * excite), bf),
            pltpu.VMEM((n + 1, rank // 2, 2 * excite), bf),
            pltpu.VMEM((n, rank // 2, 2 * excite), bf),
            pltpu.VMEM((n, rank // 2, 2 * excite), bf),
            pltpu.VMEM((far_slots + 1, rank // 2, 2 * excite), bf),
            pltpu.VMEM((far_slots * rank, excite), f32),
            pltpu.VMEM((excite, panels), f32),
            pltpu.VMEM((excite, panels), f32),
            pltpu.SemaphoreType.DMA((5,)),
            pltpu.SemaphoreType.DMA((2,)),
            pltpu.SemaphoreType.DMA((2, 2, groups)),
            pltpu.SemaphoreType.DMA((2, 2, groups)),
            pltpu.SemaphoreType.DMA((2, n)),
            pltpu.SemaphoreType.DMA((2, n)),
        ],
        compiler_params=pltpu.CompilerParams(
            collective_id=0, has_side_effects=True, vmem_limit_bytes=60 * 1024 * 1024
        ),
    )(
        idx,
        excitation,
        leaf_field,
        near_tiles.reshape(leaves * slots, leaf, leaf),
        source_factor.reshape(far_slots * rank, panels),
        target_factor.reshape(far_slots * rank, panels),
    )


def solution(mesh):
    in_specs = (
        P(None, "panels"),
        P("panels", None, None, None),
        P("panels", None),
        P("panels"),
        P(),
        P(),
        P(None, None, "panels"),
        P(None, None, "panels"),
    )
    return jax.shard_map(
        functools.partial(shards, mesh.shape["panels"]),
        mesh=mesh,
        in_specs=in_specs,
        out_specs=P(None, None, "panels"),
        check_vma=False,
    )
```

profile of v0, /device:TPU:0, one launch (start us, length us, event | category | flops | bytes accessed | tf_op | source)
XLA Modules:
  0.0 115.5 jit_solution(18120594209737806387)
XLA Ops:
  0.0 0.7 convert_reduce_fusion
  0.7 0.1 select_reduce_fusion
  0.9 0.7 iota_compare_fusion.1
  1.5 0.9 select_reduce_fusion.1
  2.4 0.7 add_select_fusion
  3.1 0.1 copy.12
  3.2 0.1 reshape.25
  3.3 0.6 pad_add_fusion.idx_ref
  3.9 1.9 %copy.16 = bf16[8,16,8,256]{3,2,0,1:T(8,128)(2,1)} copy(bf16[8,16,8,256]{3,2,1,0:T(8,128)(2,1)} %bitcast.13) | data formatting | bytes 1048576 | tf_op jit(solution)/shard_map/reshape | solution.py:214
  5.8 104.3 %shard_map.82 = f32[5,64,4096]{2,1,0:T(8,128)} custom-call(s32[128]{0:T(128)} %pad_add_fusion.idx_ref, bf16[64,4096]{1,0:T(8,128)(2,1)} %field_hbm.1, bf16[16,64,256]{2,1,0:T(8,128)(2,1)} %bitcast.14, bf16[80,256,256]{2,1,0:T(8,128)(2,1)} %bitcast.10, bf16[512,4096]{1,0:T(8,128)(2,1)} %bitcast.11, bf16[512,4096]{1,0:T(8,128)(2,1)} %bitcast.12), custom_call_target="tpu_custom_call" | custom-call | tf_op jit(solution)/shard_map/pallas_call | solution.py:219
  110.1 5.5 %copy.18 = f32[5,64,4096]{2,1,0:T(8,128)} copy(f32[5,64,4096]{2,1,0:T(8,128)} %shard_map.82) | data formatting | bytes 10485760
  (2 shorter events, 0.0 us)
where the time goes:
time: 116 us
  Pallas kernels  104 us (90%)
  local copies, waits for them, and re-layouts  7.51 us (6%)
  other arithmetic  3.7 us (3%)
    pallas_call x1, Pallas kernels, shards(): pl.pallas_call(functools.partial(kernel, n), out_shape=jax.ShapeDtypeStru...  104 us
    unnamed x1, local copies, waits for them, and re-layouts  5.45 us

commit v1 on v0

v1 whole, which is shorter than its diff:
```python
import functools

import jax
import jax.numpy as jnp
from jax import lax
from jax.experimental import pallas as pl
from jax.experimental.pallas import tpu as pltpu
from jax.sharding import PartitionSpec as P

ITERS = 5
MESH = pl.DeviceIdType.MESH
NT = (((1,), (1,)), ((), ()))

SEND = (1, 0, 2, 3)
EARLY = 2
BUFFERS = ((0, 1), (2,), (3,))
STEPS = ((3, 2), (1,), (0,))
GROUPS = 4


def kernel(n, off_ref, cnt_ref, fsrc_ref, fcnt_ref, field_hbm, near_hbm, src_hbm, tgt_hbm, out, *scratch):
    (near, src, tgt, field, main_a, main_b, *rest) = scratch
    nbuf = len(BUFFERS)
    exts = (rest[:nbuf], rest[nbuf : 2 * nbuf])
    (
        recv_a,
        recv_b,
        outg_a,
        outg_b,
        cbuf,
        acc,
        near_tab,
        send_tab,
        recv_tab,
        load_sem,
        in_send,
        in_recv,
        ext_send,
        ext_recv,
        far_send,
        far_recv,
    ) = rest[2 * nbuf :]
    mains, recvs, outgs = (main_a, main_b), (recv_a, recv_b), (outg_a, outg_b)

    me = lax.axis_index("panels")
    core = lax.rem(me, 2)
    inner = me + 1 - 2 * core
    outer = lax.rem(me + n - 1 + 2 * core, n)
    leaves, slots = off_ref.shape
    excite, panels = field.shape
    leaf = panels // leaves
    size = leaves // GROUPS
    pack = cbuf.shape[1]
    far_slots = cbuf.shape[0] - 1
    half = far_slots * pack
    last = ITERS - 1

    barrier = pltpu.get_barrier_semaphore()

    @pl.loop(1, n)
    def _(d):
        pl.semaphore_signal(barrier, inc=1, device_id=(lax.rem(me + d, n),), device_id_type=MESH)

    load_field = pltpu.make_async_copy(field_hbm, field, load_sem.at[0])
    load_src = [
        pltpu.make_async_copy(src_hbm.at[:, pl.ds(h * pack, pack), :], src.at[h], load_sem.at[1 + h]) for h in range(2)
    ]
    load_tgt = [
        pltpu.make_async_copy(tgt_hbm.at[:, pl.ds(h * pack, pack), :], tgt.at[h], load_sem.at[3 + h]) for h in range(2)
    ]
    load_near = pltpu.make_async_copy(near_hbm, near, load_sem.at[5])
    for load in [load_field, *load_src, load_near, *load_tgt]:
        load.start()

    def base(group):
        return jnp.where(core == 1, leaves - (group + 1) * size, group * size)

    def columns(group):
        return pl.ds(pl.multiple_of(base(group) * leaf, size * leaf), size * leaf)

    def inner_copy(k, group):
        own = mains[k % 2]
        return pltpu.make_async_remote_copy(
            src_ref=own.at[pl.ds(base(group), size)],
            dst_ref=own.at[pl.ds(leaves + base(group), size)],
            send_sem=in_send.at[k % 2, group],
            recv_sem=in_recv.at[k % 2, group],
            device_id=(inner,),
            device_id_type=MESH,
        )

    def outer_copy(k, place):
        buffer = next(b for b, places in enumerate(BUFFERS) if place in places)
        return pltpu.make_async_remote_copy(
            src_ref=mains[k % 2].at[pl.ds(base(SEND[place]), size)],
            dst_ref=exts[k % 2][buffer].at[pl.ds(BUFFERS[buffer].index(place) * size, size)],
            send_sem=ext_send.at[k % 2, place],
            recv_sem=ext_recv.at[k % 2, place],
            device_id=(outer,),
            device_id_type=MESH,
        )

    def far_copy(k, d):
        peer = lax.rem(me + d, n)
        return pltpu.make_async_remote_copy(
            src_ref=outgs[k % 2].at[peer],
            dst_ref=recvs[k % 2].at[me],
            send_sem=far_send.at[k % 2, d],
            recv_sem=far_recv.at[k % 2, d],
            device_id=(peer,),
            device_id_type=MESH,
        )

    blank = jnp.zeros((excite, leaf), jnp.bfloat16)
    for buffers in (mains, *exts):
        for buffer in buffers:
            buffer[buffer.shape[0] - 1] = blank
    for recv in recvs:
        recv[n] = jnp.zeros((pack, 2 * excite), jnp.bfloat16)
        recv[me] = jnp.zeros((pack, 2 * excite), jnp.bfloat16)
    cbuf[far_slots] = jnp.zeros((pack, 2 * excite), jnp.bfloat16)

    load_field.wait()
    for i in range(leaves):
        main_a[i] = field[:, i * leaf : (i + 1) * leaf]
    pl.semaphore_wait(barrier, n - 1)
    for place in range(EARLY):
        outer_copy(0, place).start()
    for group in range(GROUPS):
        inner_copy(0, group).start()

    @pl.loop(0, leaves)
    def _(i):
        for j in range(slots):
            at = i + off_ref[i, j]
            live = j < cnt_ref[i]
            low, high = at < 0, at >= leaves
            far_side = jnp.where(core == 1, high.astype(jnp.int32), low.astype(jnp.int32)) == 1
            spot = jnp.where(low, at + leaves, jnp.where(high, at - leaves, at))
            own = jnp.logical_not(jnp.logical_or(low, high))
            near_side = jnp.where(own, spot, leaves + spot)
            use = jnp.logical_and(live, jnp.logical_not(far_side))
            near_tab[i * slots + j] = jnp.where(use, near_side, 2 * leaves)
            use = jnp.logical_and(live, far_side)
            for b, places in enumerate(BUFFERS):
                found = len(places) * size
                for order, place in enumerate(places):
                    group = SEND[place]
                    first = jnp.where(core == 1, group * size, leaves - (group + 1) * size)
                    inside = jnp.logical_and(spot >= first, spot < first + size)
                    inside = jnp.logical_and(inside, use)
                    found = jnp.where(inside, order * size + spot - first, found)
                near_tab[((b + 1) * leaves + i) * slots + j] = found

    def count(t, before):
        mine = 0
        live = fcnt_ref[t]
        for j in range(far_slots):
            mine += jnp.logical_and(fsrc_ref[t, j] == me, j < live).astype(jnp.int32)
        send_tab[t] = jnp.where(mine > 0, before, far_slots)
        return before + mine

    lax.fori_loop(0, n, count, jnp.int32(0))
    my_live = fcnt_ref[me]
    for j in range(far_slots):
        recv_tab[j] = jnp.where(j < my_live, fsrc_ref[me, j], n)

    def project(group, fresh):
        cols = columns(group)
        charges = field[:, cols]
        for h in range(2):
            part = lax.dot_general(
                src[h, :, :, cols].reshape(half, size * leaf), charges, NT, preferred_element_type=jnp.float32
            )
            acc[h] = part if fresh else acc[h] + part

    def send_far(k):
        both = jnp.concatenate([acc[0], acc[1]], axis=1)
        cbuf[:far_slots] = both.reshape(far_slots, pack, 2 * excite).astype(jnp.bfloat16)
        outg = outgs[k % 2]

        @pl.loop(0, n)
        def _(t):
            outg[t] = cbuf[send_tab[t]]

        @pl.loop(1, n)
        def _(d):
            far_copy(k, d).start()

        for place in range(EARLY, GROUPS):
            outer_copy(k, place).start()

    def near_sum(k, group, step):
        own, ext = mains[k % 2], exts[k % 2][: step + 1]
        sums = []
        for u in range(size):
            i = base(group) + u
            total = None
            for j in range(slots):
                x = own[near_tab[i * slots + j]]
                for b, buffer in enumerate(ext):
                    x += buffer[near_tab[((b + 1) * leaves + i) * slots + j]]
                part = lax.dot_general(x, near[i, j], NT, preferred_element_type=jnp.float32)
                total = part if total is None else total + part
            sums.append(total)
        return jnp.concatenate(sums, axis=1)

    def finish(k, group, total):
        cols = columns(group)
        out[k, :, cols] = total
        if k < last:
            rounded = total.astype(jnp.bfloat16)
            field[:, cols] = rounded
            for u in range(size):
                mains[(k + 1) % 2][base(group) + u] = rounded[:, u * leaf : (u + 1) * leaf]

    for load in load_src:
        load.wait()
    for group in range(GROUPS):
        project(group, group == 0)
    send_far(0)

    for k in range(ITERS):
        for group in range(GROUPS):
            inner_copy(k, group).wait_recv()
        for place in BUFFERS[0]:
            outer_copy(k, place).wait_recv()
        if k == 0:
            load_near.wait()
        for group in STEPS[0]:
            out[k, :, columns(group)] = near_sum(k, group, 0)

        @pl.loop(1, n)
        def _(d):
            far_copy(k, d).wait()

        got = jnp.concatenate([recvs[k % 2][recv_tab[j]] for j in range(far_slots)], axis=0)
        got = got.astype(jnp.float32).T.astype(jnp.bfloat16)
        coef = jnp.concatenate([got[:excite], got[excite:]], axis=1)
        if k == 0:
            for load in load_tgt:
                load.wait()
        if 1 <= k < last:
            for place in range(GROUPS):
                outer_copy(k - 1, place).wait_send()
            for group in range(GROUPS):
                inner_copy(k - 1, group).wait_send()

        def far_sum(group):
            cols = columns(group)
            return jnp.dot(coef, tgt[:, :, :, cols].reshape(2 * half, size * leaf), preferred_element_type=jnp.float32)

        for group in STEPS[0]:
            finish(k, group, out[k, :, columns(group)] + far_sum(group))
            if k < last:
                inner_copy(k + 1, group).start()
        for step in STEPS[1:]:
            for group in step:
                out[k, :, columns(group)] = far_sum(group)
        if k < last:
            for at, group in enumerate(STEPS[0]):
                project(group, at == 0)
        for step in range(1, nbuf):
            for place in BUFFERS[step]:
                outer_copy(k, place).wait_recv()
            for group in STEPS[step]:
                finish(k, group, near_sum(k, group, step) + out[k, :, columns(group)])
                if k < last:
                    if group in SEND[:EARLY]:
                        outer_copy(k + 1, SEND.index(group)).start()
                    inner_copy(k + 1, group).start()
                    project(group, False)
        if k < last:
            send_far(k + 1)
    for k in range(max(ITERS - 2, 0), ITERS):
        for place in range(GROUPS):
            outer_copy(k, place).wait_send()
        for group in range(GROUPS):
            inner_copy(k, group).wait_send()


def shards(n, excitation, near_tiles, near_offset, near_count, far_src, far_count, source_factor, target_factor):
    excite, panels = excitation.shape
    leaves, slots, leaf, _ = near_tiles.shape
    far_slots, rank, _ = source_factor.shape
    size, pack = leaves // GROUPS, rank // 2
    bf, f32 = jnp.bfloat16, jnp.float32
    hbm = pl.BlockSpec(memory_space=pltpu.HBM)
    smem = pl.BlockSpec(memory_space=pltpu.SMEM)
    ext = [pltpu.VMEM((len(places) * size + 1, excite, leaf), bf) for places in BUFFERS]
    return pl.pallas_call(
        functools.partial(kernel, n),
        out_shape=pltpu.VMEM((ITERS, excite, panels), f32),
        in_specs=[smem] * 4 + [hbm] * 4,
        out_specs=pl.BlockSpec(memory_space=pltpu.VMEM),
        scratch_shapes=[
            pltpu.VMEM((leaves, slots, leaf, leaf), bf),
            pltpu.VMEM((2, far_slots, pack, panels), bf),
            pltpu.VMEM((2, far_slots, pack, panels), bf),
            pltpu.VMEM((excite, panels), bf),
            pltpu.VMEM((2 * leaves + 1, excite, leaf), bf),
            pltpu.VMEM((2 * leaves + 1, excite, leaf), bf),
            *ext,
            *ext,
            pltpu.VMEM((n + 1, pack, 2 * excite), bf),
            pltpu.VMEM((n + 1, pack, 2 * excite), bf),
            pltpu.VMEM((n, pack, 2 * excite), bf),
            pltpu.VMEM((n, pack, 2 * excite), bf),
            pltpu.VMEM((far_slots + 1, pack, 2 * excite), bf),
            pltpu.VMEM((2, far_slots * pack, excite), f32),
            pltpu.SMEM(((1 + len(BUFFERS)) * leaves * slots,), jnp.int32),
            pltpu.SMEM((n,), jnp.int32),
            pltpu.SMEM((far_slots,), jnp.int32),
            pltpu.SemaphoreType.DMA((6,)),
            pltpu.SemaphoreType.DMA((2, GROUPS)),
            pltpu.SemaphoreType.DMA((2, GROUPS)),
            pltpu.SemaphoreType.DMA((2, GROUPS)),
            pltpu.SemaphoreType.DMA((2, GROUPS)),
            pltpu.SemaphoreType.DMA((2, n)),
            pltpu.SemaphoreType.DMA((2, n)),
        ],
        compiler_params=pltpu.CompilerParams(
            collective_id=0, has_side_effects=True, vmem_limit_bytes=54 * 1024 * 1024
        ),
    )(near_offset, near_count, far_src, far_count, excitation, near_tiles, source_factor, target_factor)


def solution(mesh):
    in_specs = (
        P(None, "panels"),
        P("panels", None, None, None),
        P("panels", None),
        P("panels"),
        P(),
        P(),
        P(None, None, "panels"),
        P(None, None, "panels"),
    )
    return jax.shard_map(
        functools.partial(shards, mesh.shape["panels"]),
        mesh=mesh,
        in_specs=in_specs,
        out_specs=P(None, None, "panels"),
        check_vma=False,
    )
```

time: 116 us -> 91.1 us (0.79)
  Pallas kernels: 104 us -> 85.8 us
  other arithmetic: 3.7 us -> 0 us
  local copies, waits for them, and re-layouts: 7.51 us -> 5.09 us
    pallas_call x1, Pallas kernels: 104 us -> 85.8 us  [shards(): pl.pallas_call(functools.partial(kernel, n), out_shape=pltpu.VMEM((ITERS,...]
    reshape x2 -> x0, local copies, waits for them, and re-layouts: 1.97 us -> none  [the longest x1 1.89 us: shards(): leaf_field = excitation.reshape(excite, leaves, leaf).transpose(1, 0, 2)]
    select_n x3 -> x0, other arithmetic: 1.58 us -> none  [the longest x1 0.88 us: shards(): recv_idx = jnp.where(my_live, my_src, n)]
    unnamed x1 -> x3, local copies, waits for them, and re-layouts: 5.45 us -> 5.09 us
where the time goes in v1:
time: 91.1 us; the launch traced here: 90.9 us
  Pallas kernels  85.8 us (94%)
  local copies, waits for them, and re-layouts  5.09 us (6%)
    pallas_call x1, Pallas kernels, shards(): pl.pallas_call(functools.partial(kernel, n), out_shape=pltpu.VMEM((ITERS,...  85.8 us
    unnamed x3, local copies, waits for them, and re-layouts  5.09 us

profile of v1, /device:TPU:0, one launch (start us, length us, event | category | flops | bytes accessed | tf_op | source)
XLA Modules:
  0.0 90.9 jit_solution(11167337307425183177)
XLA Ops:
  0.0 1.4 %copy.9.off_ref = s32[16,5]{1,0:T(8,128)} copy(s32[16,5]{0,1:T(8,128)} %param.10) | data formatting | bytes 640 | tf_op args[2]
  1.4 1.4 %copy.10.fsrc_ref = s32[32,16]{1,0:T(8,128)} copy(s32[32,16]{0,1:T(8,128)} %param.12) | data formatting | bytes 4096 | tf_op args[4]
  2.7 85.8 %shard_map.82 = f32[5,64,4096]{2,1,0:T(8,128)S(1)} custom-call(s32[16,5]{1,0:T(8,128)} %copy.9.off_ref, s32[16]{0:T(128)} %cnt_ref.1, s32[32,16]{1,0:T(8,128)} %copy.10.fsrc_ref, s32[32]{0:T(128)} %fcnt_ref.1, bf16[64,4096]{1,0:T(8,128)(2,1)} %field_hbm.1, bf16[16,5,256,256]{3,2,1,0:T(8,128)(2,1)} %near_hbm.1, bf16[16,32,4096]{2,1,0:T(8,128)(2,1)} %src_hbm.1, ...), custom_call_target="tpu_custom_call" | custom-call | tf_op jit(solution)/shard_map/pallas_call | solution.py:291
  88.5 2.4 %copy.12 = f32[5,64,4096]{2,1,0:T(8,128)} copy(f32[5,64,4096]{2,1,0:T(8,128)S(1)} %shard_map.82) | data formatting | bytes 10485760

commit v2 on v1

--- a/solution.py
+++ b/solution.py
@@ -12,14 +12,13 @@
 NT = (((1,), (1,)), ((), ()))
 
 SEND = (1, 0, 2, 3)
-EARLY = 2
 BUFFERS = ((0, 1), (2,), (3,))
-STEPS = ((3, 2), (1,), (0,))
+NEED = (2, 1, 0, 0)
 GROUPS = 4
 
 
-def kernel(n, off_ref, cnt_ref, fsrc_ref, fcnt_ref, field_hbm, near_hbm, src_hbm, tgt_hbm, out, *scratch):
-    (near, src, tgt, field, main_a, main_b, *rest) = scratch
+def kernel(n, off_hbm, cnt_hbm, fsrc_hbm, fcnt_hbm, field_hbm, near_hbm, src_hbm, tgt_hbm, out, *scratch):
+    off_ref, cnt_ref, fsrc_ref, fcnt_ref, near, src, tgt, field, main_a, main_b, *rest = scratch
     nbuf = len(BUFFERS)
     exts = (rest[:nbuf], rest[nbuf : 2 * nbuf])
     (
@@ -46,7 +45,7 @@
     core = lax.rem(me, 2)
     inner = me + 1 - 2 * core
     outer = lax.rem(me + n - 1 + 2 * core, n)
-    leaves, slots = off_ref.shape
+    slots, leaves = off_ref.shape
     excite, panels = field.shape
     leaf = panels // leaves
     size = leaves // GROUPS
@@ -69,7 +68,13 @@
         pltpu.make_async_copy(tgt_hbm.at[:, pl.ds(h * pack, pack), :], tgt.at[h], load_sem.at[3 + h]) for h in range(2)
     ]
     load_near = pltpu.make_async_copy(near_hbm, near, load_sem.at[5])
-    for load in [load_field, *load_src, load_near, *load_tgt]:
+    load_ints = [
+        pltpu.make_async_copy(a, b, load_sem.at[6 + i])
+        for i, (a, b) in enumerate(
+            ((off_hbm, off_ref), (cnt_hbm, cnt_ref), (fsrc_hbm, fsrc_ref), (fcnt_hbm, fcnt_ref))
+        )
+    ]
+    for load in [load_field, *load_ints, *load_src, load_near, *load_tgt]:
         load.start()
 
     def base(group):
@@ -120,50 +125,54 @@
         recv[me] = jnp.zeros((pack, 2 * excite), jnp.bfloat16)
     cbuf[far_slots] = jnp.zeros((pack, 2 * excite), jnp.bfloat16)
 
+    for load in load_ints:
+        load.wait()
+
+    def count(t, before):
+        mine = 0
+        live = fcnt_ref[t]
+        for j in range(far_slots):
+            mine += jnp.logical_and(fsrc_ref[j, t] == me, j < live).astype(jnp.int32)
+        send_tab[t] = jnp.where(mine > 0, before, far_slots)
+        return before + mine
+
+    lax.fori_loop(0, n, count, jnp.int32(0))
+    my_live = fcnt_ref[me]
+    for j in range(far_slots):
+        recv_tab[j] = jnp.where(j < my_live, fsrc_ref[j, me], n)
+
     load_field.wait()
     for i in range(leaves):
         main_a[i] = field[:, i * leaf : (i + 1) * leaf]
     pl.semaphore_wait(barrier, n - 1)
-    for place in range(EARLY):
+    for place in (0, 1):
         outer_copy(0, place).start()
     for group in range(GROUPS):
         inner_copy(0, group).start()
 
-    @pl.loop(0, leaves)
-    def _(i):
-        for j in range(slots):
-            at = i + off_ref[i, j]
-            live = j < cnt_ref[i]
-            low, high = at < 0, at >= leaves
-            far_side = jnp.where(core == 1, high.astype(jnp.int32), low.astype(jnp.int32)) == 1
-            spot = jnp.where(low, at + leaves, jnp.where(high, at - leaves, at))
-            own = jnp.logical_not(jnp.logical_or(low, high))
-            near_side = jnp.where(own, spot, leaves + spot)
-            use = jnp.logical_and(live, jnp.logical_not(far_side))
-            near_tab[i * slots + j] = jnp.where(use, near_side, 2 * leaves)
-            use = jnp.logical_and(live, far_side)
-            for b, places in enumerate(BUFFERS):
-                found = len(places) * size
-                for order, place in enumerate(places):
-                    group = SEND[place]
-                    first = jnp.where(core == 1, group * size, leaves - (group + 1) * size)
-                    inside = jnp.logical_and(spot >= first, spot < first + size)
-                    inside = jnp.logical_and(inside, use)
-                    found = jnp.where(inside, order * size + spot - first, found)
-                near_tab[((b + 1) * leaves + i) * slots + j] = found
-
-    def count(t, before):
-        mine = 0
-        live = fcnt_ref[t]
-        for j in range(far_slots):
-            mine += jnp.logical_and(fsrc_ref[t, j] == me, j < live).astype(jnp.int32)
-        send_tab[t] = jnp.where(mine > 0, before, far_slots)
-        return before + mine
-
-    lax.fori_loop(0, n, count, jnp.int32(0))
-    my_live = fcnt_ref[me]
-    for j in range(far_slots):
-        recv_tab[j] = jnp.where(j < my_live, fsrc_ref[me, j], n)
+    def near_table():
+        @pl.loop(0, leaves)
+        def _(i):
+            for j in range(slots):
+                at = i + off_ref[j, i]
+                live = j < cnt_ref[i]
+                low, high = at < 0, at >= leaves
+                far_side = jnp.where(core == 1, high.astype(jnp.int32), low.astype(jnp.int32)) == 1
+                spot = jnp.where(low, at + leaves, jnp.where(high, at - leaves, at))
+                own = jnp.logical_not(jnp.logical_or(low, high))
+                near_side = jnp.where(own, spot, leaves + spot)
+                use = jnp.logical_and(live, jnp.logical_not(far_side))
+                near_tab[i * slots + j] = jnp.where(use, near_side, 2 * leaves)
+                use = jnp.logical_and(live, far_side)
+                for b, places in enumerate(BUFFERS):
+                    found = len(places) * size
+                    for order, place in enumerate(places):
+                        group = SEND[place]
+                        first = jnp.where(core == 1, group * size, leaves - (group + 1) * size)
+                        inside = jnp.logical_and(spot >= first, spot < first + size)
+                        inside = jnp.logical_and(inside, use)
+                        found = jnp.where(inside, order * size + spot - first, found)
+                    near_tab[((b + 1) * leaves + i) * slots + j] = found
 
     def project(group, fresh):
         cols = columns(group)
@@ -187,11 +196,8 @@
         def _(d):
             far_copy(k, d).start()
 
-        for place in range(EARLY, GROUPS):
-            outer_copy(k, place).start()
-
-    def near_sum(k, group, step):
-        own, ext = mains[k % 2], exts[k % 2][: step + 1]
+    def near_sum(k, group):
+        own, ext = mains[k % 2], exts[k % 2][: NEED[group] + 1]
         sums = []
         for u in range(size):
             i = base(group) + u
@@ -200,10 +206,14 @@
                 x = own[near_tab[i * slots + j]]
                 for b, buffer in enumerate(ext):
                     x += buffer[near_tab[((b + 1) * leaves + i) * slots + j]]
-                part = lax.dot_general(x, near[i, j], NT, preferred_element_type=jnp.float32)
+                part = jnp.dot(x, near[i, j], preferred_element_type=jnp.float32)
                 total = part if total is None else total + part
             sums.append(total)
         return jnp.concatenate(sums, axis=1)
+
+    def far_sum(coef, group):
+        rows = tgt[:, :, :, columns(group)].reshape(2 * half, size * leaf)
+        return jnp.dot(coef, rows, preferred_element_type=jnp.float32)
 
     def finish(k, group, total):
         cols = columns(group)
@@ -213,22 +223,65 @@
             field[:, cols] = rounded
             for u in range(size):
                 mains[(k + 1) % 2][base(group) + u] = rounded[:, u * leaf : (u + 1) * leaf]
+            inner_copy(k + 1, group).start()
+            if group in SEND[:2]:
+                outer_copy(k + 1, SEND.index(group)).start()
+
+    def wait_sent(k):
+        for place in range(GROUPS):
+            outer_copy(k, place).wait_send()
+        for group in range(GROUPS):
+            inner_copy(k, group).wait_send()
 
     for load in load_src:
         load.wait()
     for group in range(GROUPS):
         project(group, group == 0)
-    send_far(0)
 
     for k in range(ITERS):
+        part = {}
+
+        def add_near(group):
+            part[group] = True
+            cols = columns(group)
+            total = near_sum(k, group)
+            if group in far_done:
+                finish(k, group, total + out[k, :, cols])
+            else:
+                out[k, :, cols] = total
+
+        def add_far(coef, group):
+            far_done.add(group)
+            cols = columns(group)
+            total = far_sum(coef, group)
+            if group in part:
+                finish(k, group, total + out[k, :, cols])
+            else:
+                out[k, :, cols] = total
+
+        far_done = set()
+        send_far(k)
+        outer_copy(k, 2).start()
+        outer_copy(k, 3).start()
+        if k == 0:
+            near_table()
+            load_near.wait()
+
+            @pl.loop(0, leaves)
+            def _(i):
+                for j in range(slots):
+                    near[i, j] = near[i, j].T
+
         for group in range(GROUPS):
             inner_copy(k, group).wait_recv()
-        for place in BUFFERS[0]:
+        for place in (0, 1):
             outer_copy(k, place).wait_recv()
-        if k == 0:
-            load_near.wait()
-        for group in STEPS[0]:
-            out[k, :, columns(group)] = near_sum(k, group, 0)
+        add_near(3)
+        if k < last:
+            outer_copy(k, 2).wait_recv()
+            add_near(1)
+        else:
+            add_near(2)
 
         @pl.loop(1, n)
         def _(d):
@@ -241,42 +294,26 @@
             for load in load_tgt:
                 load.wait()
         if 1 <= k < last:
-            for place in range(GROUPS):
-                outer_copy(k - 1, place).wait_send()
-            for group in range(GROUPS):
-                inner_copy(k - 1, group).wait_send()
-
-        def far_sum(group):
-            cols = columns(group)
-            return jnp.dot(coef, tgt[:, :, :, cols].reshape(2 * half, size * leaf), preferred_element_type=jnp.float32)
-
-        for group in STEPS[0]:
-            finish(k, group, out[k, :, columns(group)] + far_sum(group))
-            if k < last:
-                inner_copy(k + 1, group).start()
-        for step in STEPS[1:]:
-            for group in step:
-                out[k, :, columns(group)] = far_sum(group)
+            wait_sent(k - 1)
         if k < last:
-            for at, group in enumerate(STEPS[0]):
+            add_far(coef, 1)
+            add_far(coef, 0)
+            add_near(2)
+            outer_copy(k, 3).wait_recv()
+            add_near(0)
+            add_far(coef, 3)
+            add_far(coef, 2)
+            for at, group in enumerate((1, 3, 2, 0)):
                 project(group, at == 0)
-        for step in range(1, nbuf):
-            for place in BUFFERS[step]:
-                outer_copy(k, place).wait_recv()
-            for group in STEPS[step]:
-                finish(k, group, near_sum(k, group, step) + out[k, :, columns(group)])
-                if k < last:
-                    if group in SEND[:EARLY]:
-                        outer_copy(k + 1, SEND.index(group)).start()
-                    inner_copy(k + 1, group).start()
-                    project(group, False)
-        if k < last:
-            send_far(k + 1)
+        else:
+            for group in (3, 2, 1, 0):
+                add_far(coef, group)
+            outer_copy(k, 2).wait_recv()
+            add_near(1)
+            outer_copy(k, 3).wait_recv()
+            add_near(0)
     for k in range(max(ITERS - 2, 0), ITERS):
-        for place in range(GROUPS):
-            outer_copy(k, place).wait_send()
-        for group in range(GROUPS):
-            inner_copy(k, group).wait_send()
+        wait_sent(k)
 
 
 def shards(n, excitation, near_tiles, near_offset, near_count, far_src, far_count, source_factor, target_factor):
@@ -286,14 +323,17 @@
     size, pack = leaves // GROUPS, rank // 2
     bf, f32 = jnp.bfloat16, jnp.float32
     hbm = pl.BlockSpec(memory_space=pltpu.HBM)
-    smem = pl.BlockSpec(memory_space=pltpu.SMEM)
     ext = [pltpu.VMEM((len(places) * size + 1, excite, leaf), bf) for places in BUFFERS]
     return pl.pallas_call(
         functools.partial(kernel, n),
         out_shape=pltpu.VMEM((ITERS, excite, panels), f32),
-        in_specs=[smem] * 4 + [hbm] * 4,
+        in_specs=[hbm] * 8,
         out_specs=pl.BlockSpec(memory_space=pltpu.VMEM),
         scratch_shapes=[
+            pltpu.SMEM((slots, leaves), jnp.int32),
+            pltpu.SMEM((leaves,), jnp.int32),
+            pltpu.SMEM((far_slots, n), jnp.int32),
+            pltpu.SMEM((n,), jnp.int32),
             pltpu.VMEM((leaves, slots, leaf, leaf), bf),
             pltpu.VMEM((2, far_slots, pack, panels), bf),
             pltpu.VMEM((2, far_slots, pack, panels), bf),
@@ -311,7 +351,7 @@
             pltpu.SMEM(((1 + len(BUFFERS)) * leaves * slots,), jnp.int32),
             pltpu.SMEM((n,), jnp.int32),
             pltpu.SMEM((far_slots,), jnp.int32),
-            pltpu.SemaphoreType.DMA((6,)),
+            pltpu.SemaphoreType.DMA((10,)),
             pltpu.SemaphoreType.DMA((2, GROUPS)),
             pltpu.SemaphoreType.DMA((2, GROUPS)),
             pltpu.SemaphoreType.DMA((2, GROUPS)),
@@ -322,7 +362,7 @@
         compiler_params=pltpu.CompilerParams(
             collective_id=0, has_side_effects=True, vmem_limit_bytes=54 * 1024 * 1024
         ),
-    )(near_offset, near_count, far_src, far_count, excitation, near_tiles, source_factor, target_factor)
+    )(near_offset.T, near_count, far_src.T, far_count, excitation, near_tiles, source_factor, target_factor)
 
 
 def solution(mesh):

time: 91.1 us -> 79.7 us (0.87)
  Pallas kernels: 85.8 us -> 77.2 us
  local copies, waits for them, and re-layouts: 5.09 us -> 2.36 us
    pallas_call x1, Pallas kernels: 85.8 us -> 77.2 us  [shards(): pl.pallas_call(functools.partial(kernel, n), out_shape=pltpu.VMEM((ITERS,...]
    unnamed x3 -> x1, local copies, waits for them, and re-layouts: 5.09 us -> 2.36 us
where the time goes in v2:
time: 79.7 us; the launch traced here: 79.5 us
  Pallas kernels  77.2 us (97%)
  local copies, waits for them, and re-layouts  2.36 us (3%)
    pallas_call x1, Pallas kernels, shards(): pl.pallas_call(functools.partial(kernel, n), out_shape=pltpu.VMEM((ITERS,...  77.2 us
    unnamed x1, local copies, waits for them, and re-layouts  2.36 us

profile of v2, /device:TPU:0, one launch (start us, length us, event | category | flops | bytes accessed | tf_op | source)
XLA Modules:
  0.0 79.5 jit_solution(596706273544030856)
XLA Ops:
  0.0 77.2 %shard_map.82 = f32[5,64,4096]{2,1,0:T(8,128)S(1)} custom-call(s32[5,16]{1,0:T(8,128)} %bitcast.3, s32[16]{0:T(128)} %cnt_hbm.1, s32[16,32]{1,0:T(8,128)} %bitcast.2, s32[32]{0:T(128)} %fcnt_hbm.1, bf16[64,4096]{1,0:T(8,128)(2,1)} %field_hbm.1, bf16[16,5,256,256]{3,2,1,0:T(8,128)(2,1)} %near_hbm.1, bf16[16,32,4096]{2,1,0:T(8,128)(2,1)} %src_hbm.1, ...), custom_call_target="tpu_custom_call" | custom-call | tf_op jit(solution)/shard_map/pallas_call | solution.py:327
  77.2 2.4 %copy.10 = f32[5,64,4096]{2,1,0:T(8,128)} copy(f32[5,64,4096]{2,1,0:T(8,128)S(1)} %shard_map.82) | data formatting | bytes 10485760

commit v3 on v2

--- a/solution.py
+++ b/solution.py
@@ -56,11 +56,13 @@
 
     barrier = pltpu.get_barrier_semaphore()
 
+    load_field = pltpu.make_async_copy(field_hbm, field, load_sem.at[0])
+    load_field.start()
+
     @pl.loop(1, n)
     def _(d):
         pl.semaphore_signal(barrier, inc=1, device_id=(lax.rem(me + d, n),), device_id_type=MESH)
 
-    load_field = pltpu.make_async_copy(field_hbm, field, load_sem.at[0])
     load_src = [
         pltpu.make_async_copy(src_hbm.at[:, pl.ds(h * pack, pack), :], src.at[h], load_sem.at[1 + h]) for h in range(2)
     ]
@@ -74,7 +76,7 @@
             ((off_hbm, off_ref), (cnt_hbm, cnt_ref), (fsrc_hbm, fsrc_ref), (fcnt_hbm, fcnt_ref))
         )
     ]
-    for load in [load_field, *load_ints, *load_src, load_near, *load_tgt]:
+    for load in [*load_ints, *load_src]:
         load.start()
 
     def base(group):
@@ -82,14 +84,17 @@
 
     def columns(group):
         return pl.ds(pl.multiple_of(base(group) * leaf, size * leaf), size * leaf)
+
+    def taken(ref, sem):
+        pltpu.make_async_copy(ref, ref, sem).wait()
 
     def inner_copy(k, group):
         own = mains[k % 2]
         return pltpu.make_async_remote_copy(
             src_ref=own.at[pl.ds(base(group), size)],
             dst_ref=own.at[pl.ds(leaves + base(group), size)],
-            send_sem=in_send.at[k % 2, group],
-            recv_sem=in_recv.at[k % 2, group],
+            send_sem=in_send.at[k % 2],
+            recv_sem=in_recv.at[k % 2],
             device_id=(inner,),
             device_id_type=MESH,
         )
@@ -99,7 +104,7 @@
         return pltpu.make_async_remote_copy(
             src_ref=mains[k % 2].at[pl.ds(base(SEND[place]), size)],
             dst_ref=exts[k % 2][buffer].at[pl.ds(BUFFERS[buffer].index(place) * size, size)],
-            send_sem=ext_send.at[k % 2, place],
+            send_sem=ext_send.at[k % 2],
             recv_sem=ext_recv.at[k % 2, place],
             device_id=(outer,),
             device_id_type=MESH,
@@ -110,8 +115,8 @@
         return pltpu.make_async_remote_copy(
             src_ref=outgs[k % 2].at[peer],
             dst_ref=recvs[k % 2].at[me],
-            send_sem=far_send.at[k % 2, d],
-            recv_sem=far_recv.at[k % 2, d],
+            send_sem=far_send.at[k % 2],
+            recv_sem=far_recv.at[k % 2],
             device_id=(peer,),
             device_id_type=MESH,
         )
@@ -125,6 +130,17 @@
         recv[me] = jnp.zeros((pack, 2 * excite), jnp.bfloat16)
     cbuf[far_slots] = jnp.zeros((pack, 2 * excite), jnp.bfloat16)
 
+    load_field.wait()
+    for i in range(leaves):
+        main_a[i] = field[:, i * leaf : (i + 1) * leaf]
+    for load in [load_near, *load_tgt]:
+        load.start()
+    pl.semaphore_wait(barrier, n - 1)
+    for place in (0, 1):
+        outer_copy(0, place).start()
+    for group in range(GROUPS):
+        inner_copy(0, group).start()
+
     for load in load_ints:
         load.wait()
 
@@ -140,15 +156,6 @@
     my_live = fcnt_ref[me]
     for j in range(far_slots):
         recv_tab[j] = jnp.where(j < my_live, fsrc_ref[j, me], n)
-
-    load_field.wait()
-    for i in range(leaves):
-        main_a[i] = field[:, i * leaf : (i + 1) * leaf]
-    pl.semaphore_wait(barrier, n - 1)
-    for place in (0, 1):
-        outer_copy(0, place).start()
-    for group in range(GROUPS):
-        inner_copy(0, group).start()
 
     def near_table():
         @pl.loop(0, leaves)
@@ -194,7 +201,7 @@
 
         @pl.loop(1, n)
         def _(d):
-            far_copy(k, d).start()
+            far_copy(k, n - d).start()
 
     def near_sum(k, group):
         own, ext = mains[k % 2], exts[k % 2][: NEED[group] + 1]
@@ -228,10 +235,9 @@
                 outer_copy(k + 1, SEND.index(group)).start()
 
     def wait_sent(k):
-        for place in range(GROUPS):
-            outer_copy(k, place).wait_send()
-        for group in range(GROUPS):
-            inner_copy(k, group).wait_send()
+        own = mains[k % 2].at[pl.ds(0, leaves)]
+        taken(own, ext_send.at[k % 2])
+        taken(own, in_send.at[k % 2])
 
     for load in load_src:
         load.wait()
@@ -272,20 +278,17 @@
                 for j in range(slots):
                     near[i, j] = near[i, j].T
 
-        for group in range(GROUPS):
-            inner_copy(k, group).wait_recv()
+        taken(mains[k % 2].at[pl.ds(0, leaves)], in_recv.at[k % 2])
         for place in (0, 1):
             outer_copy(k, place).wait_recv()
         add_near(3)
-        if k < last:
-            outer_copy(k, 2).wait_recv()
-            add_near(1)
-        else:
-            add_near(2)
-
-        @pl.loop(1, n)
-        def _(d):
-            far_copy(k, d).wait()
+        add_near(2)
+        outer_copy(k, 2).wait_recv()
+        add_near(1)
+
+        whole = recvs[k % 2].at[pl.ds(0, n - 1)]
+        taken(whole, far_send.at[k % 2])
+        taken(whole, far_recv.at[k % 2])
 
         got = jnp.concatenate([recvs[k % 2][recv_tab[j]] for j in range(far_slots)], axis=0)
         got = got.astype(jnp.float32).T.astype(jnp.bfloat16)
@@ -298,7 +301,6 @@
         if k < last:
             add_far(coef, 1)
             add_far(coef, 0)
-            add_near(2)
             outer_copy(k, 3).wait_recv()
             add_near(0)
             add_far(coef, 3)
@@ -308,8 +310,6 @@
         else:
             for group in (3, 2, 1, 0):
                 add_far(coef, group)
-            outer_copy(k, 2).wait_recv()
-            add_near(1)
             outer_copy(k, 3).wait_recv()
             add_near(0)
     for k in range(max(ITERS - 2, 0), ITERS):
@@ -352,12 +352,12 @@
             pltpu.SMEM((n,), jnp.int32),
             pltpu.SMEM((far_slots,), jnp.int32),
             pltpu.SemaphoreType.DMA((10,)),
+            pltpu.SemaphoreType.DMA((2,)),
+            pltpu.SemaphoreType.DMA((2,)),
+            pltpu.SemaphoreType.DMA((2,)),
             pltpu.SemaphoreType.DMA((2, GROUPS)),
-            pltpu.SemaphoreType.DMA((2, GROUPS)),
-            pltpu.SemaphoreType.DMA((2, GROUPS)),
-            pltpu.SemaphoreType.DMA((2, GROUPS)),
-            pltpu.SemaphoreType.DMA((2, n)),
-            pltpu.SemaphoreType.DMA((2, n)),
+            pltpu.SemaphoreType.DMA((2,)),
+            pltpu.SemaphoreType.DMA((2,)),
         ],
         compiler_params=pltpu.CompilerParams(
             collective_id=0, has_side_effects=True, vmem_limit_bytes=54 * 1024 * 1024

time: 79.7 us -> 76.2 us (0.956)
  Pallas kernels: 77.2 us -> 73 us
    pallas_call x1, Pallas kernels: 77.2 us -> 73 us  [shards(): pl.pallas_call(functools.partial(kernel, n), out_shape=pltpu.VMEM((ITERS,...]
where the time goes in v3:
time: 76.2 us; the launch traced here: 75.3 us
  Pallas kernels  73 us (96%)
  local copies, waits for them, and re-layouts  2.36 us (3%)
    pallas_call x1, Pallas kernels, shards(): pl.pallas_call(functools.partial(kernel, n), out_shape=pltpu.VMEM((ITERS,...  73 us
    unnamed x1, local copies, waits for them, and re-layouts  2.36 us

profile of v3, /device:TPU:0, one launch (start us, length us, event | category | flops | bytes accessed | tf_op | source)
XLA Modules:
  0.0 75.3 jit_solution(14869615588146642473)
XLA Ops:
  0.0 73.0 %shard_map.82 = f32[5,64,4096]{2,1,0:T(8,128)S(1)} custom-call(s32[5,16]{1,0:T(8,128)} %bitcast.3, s32[16]{0:T(128)} %cnt_hbm.1, s32[16,32]{1,0:T(8,128)} %bitcast.2, s32[32]{0:T(128)} %fcnt_hbm.1, bf16[64,4096]{1,0:T(8,128)(2,1)} %field_hbm.1, bf16[16,5,256,256]{3,2,1,0:T(8,128)(2,1)} %near_hbm.1, bf16[16,32,4096]{2,1,0:T(8,128)(2,1)} %src_hbm.1, ...), custom_call_target="tpu_custom_call" | custom-call | tf_op jit(solution)/shard_map/pallas_call | solution.py:327
  73.0 2.4 %copy.10 = f32[5,64,4096]{2,1,0:T(8,128)} copy(f32[5,64,4096]{2,1,0:T(8,128)S(1)} %shard_map.82) | data formatting | bytes 10485760

commit v4 on v3

--- a/solution.py
+++ b/solution.py
@@ -195,13 +195,17 @@
         cbuf[:far_slots] = both.reshape(far_slots, pack, 2 * excite).astype(jnp.bfloat16)
         outg = outgs[k % 2]
 
-        @pl.loop(0, n)
+        @pl.loop(0, n // 2)
         def _(t):
-            outg[t] = cbuf[send_tab[t]]
-
-        @pl.loop(1, n)
+            for u in range(2):
+                outg[2 * t + u] = cbuf[send_tab[2 * t + u]]
+
+        far_copy(k, n - 1).start()
+
+        @pl.loop(1, n // 2)
         def _(d):
-            far_copy(k, n - d).start()
+            for u in range(2):
+                far_copy(k, n - 2 * d - u).start()
 
     def near_sum(k, group):
         own, ext = mains[k % 2], exts[k % 2][: NEED[group] + 1]
@@ -301,10 +305,10 @@
         if k < last:
             add_far(coef, 1)
             add_far(coef, 0)
+            add_far(coef, 3)
+            add_far(coef, 2)
             outer_copy(k, 3).wait_recv()
             add_near(0)
-            add_far(coef, 3)
-            add_far(coef, 2)
             for at, group in enumerate((1, 3, 2, 0)):
                 project(group, at == 0)
         else:

time: 76.2 us -> 76.3 us (level)
  no operation moved by 1% of the time
where the time goes in v4:
time: 76.3 us; the launch traced here: 75.4 us
  Pallas kernels  73 us (96%)
  local copies, waits for them, and re-layouts  2.36 us (3%)
    pallas_call x1, Pallas kernels, shards(): pl.pallas_call(functools.partial(kernel, n), out_shape=pltpu.VMEM((ITERS,...  73 us
    unnamed x1, local copies, waits for them, and re-layouts  2.36 us

profile of v4, /device:TPU:0, one launch (start us, length us, event | category | flops | bytes accessed | tf_op | source)
XLA Modules:
  0.0 75.4 jit_solution(2557947688054531787)
XLA Ops:
  0.0 73.0 %shard_map.82 = f32[5,64,4096]{2,1,0:T(8,128)S(1)} custom-call(s32[5,16]{1,0:T(8,128)} %bitcast.3, s32[16]{0:T(128)} %cnt_hbm.1, s32[16,32]{1,0:T(8,128)} %bitcast.2, s32[32]{0:T(128)} %fcnt_hbm.1, bf16[64,4096]{1,0:T(8,128)(2,1)} %field_hbm.1, bf16[16,5,256,256]{3,2,1,0:T(8,128)(2,1)} %near_hbm.1, bf16[16,32,4096]{2,1,0:T(8,128)(2,1)} %src_hbm.1, ...), custom_call_target="tpu_custom_call" | custom-call | tf_op jit(solution)/shard_map/pallas_call | solution.py:331
  73.1 2.4 %copy.10 = f32[5,64,4096]{2,1,0:T(8,128)} copy(f32[5,64,4096]{2,1,0:T(8,128)S(1)} %shard_map.82) | data formatting | bytes 10485760
